TPU v7x, 32 devices: a whole 2x2x4 slice. The times are simulated.
32 devices in a mesh: wide: 16 (over z, y, x), narrow: 2 (over core).
Axes of the slice: x: 2, y: 2, z: 4, core: 2. Of those that a mesh axis runs over, the one named last changes fastest.
Arguments:
- inputs: float32 [16, 64, 16, 128], P(None, 'wide', 'narrow'), may hold values from -100 to 100
- old_basis: float32 [256, 64, 16, 128], P(None, 'wide', 'narrow'), may hold values from -12 to 12
- conductance: float32 [64, 16, 128], P('wide', 'narrow'), may hold values from 0.5 to 2
- shifts: float32 [3], replicated, may hold values from 0.2 to 4
Outputs:
- new_columns: float32 [48, 64, 16, 128], P(None, 'wide', 'narrow')
- coefficients: float32 [256, 48], replicated
- col_scale: float32 [48], replicated
All inputs are finite; a program needn't handle non-finite values.
Results may differ from a plain program's by a relative error of at most 0.00011.
Values sent between devices are 32-bit elements; how exact they have to be, the bound alone decides.
No kernel may reach another device: no remote copies, remote signals or barrier semaphores. Data moves between devices by JAX's collectives and lax.ppermute only.
A program may use at most 64 MiB of HBM per device.

v0:
```python
import jax
import jax.numpy as jnp
from jax import lax
from jax.sharding import PartitionSpec as P

ITERS = 4


def padded_2(cells, sides, width):
    for axis, dim in sides:
        count = lax.axis_size(axis)
        ends = count - 1
        head = lax.slice_in_dim(cells, 0, width, axis=dim)
        tail = lax.slice_in_dim(cells, cells.shape[dim] - width, cells.shape[dim], axis=dim)
        cells = jnp.concatenate(
            [
                lax.ppermute(tail, axis, [(i, (i + 1) % count) for i in range(ends)]),
                cells,
                lax.ppermute(head, axis, [((i + 1) % count, i) for i in range(ends)]),
            ],
            axis=dim,
        )
    return cells


def spread(coef):
    return coef[:, None, None, None]


def stencil(padded, conductance, shift_col):
    center = padded[:, 1:-1, 1:-1, :]
    deeper = jnp.pad(padded, ((0, 0), (0, 0), (0, 0), (1, 1)))
    beside_all = deeper[:, 2:, 1:-1, 1:-1] + deeper[:, :-2, 1:-1, 1:-1]
    beside_all = beside_all + deeper[:, 1:-1, 2:, 1:-1] + deeper[:, 1:-1, :-2, 1:-1]
    beside_all = beside_all + deeper[:, 1:-1, 1:-1, 2:] + deeper[:, 1:-1, 1:-1, :-2]
    return conductance[None] * (6.0 * center - beside_all) + spread(shift_col) * center


def operate(values, conductance, shift_col):
    padded = padded_2(values, (("wide", 1), ("narrow", 2)), 1)
    return stencil(padded, conductance, shift_col)


def local_dot(left, right):
    return jnp.sum(left * right, axis=(1, 2, 3))


def shards(inputs, old_basis, conductance, shifts):
    total_cells = (
        inputs.shape[1]
        * inputs.shape[2]
        * inputs.shape[3]
        * lax.axis_size("wide")
        * lax.axis_size("narrow")
    )
    shift_col = jnp.repeat(shifts, inputs.shape[0])
    shadow = jnp.tile(inputs, (shifts.shape[0], 1, 1, 1))
    columns = shadow.shape[0]
    solution = jnp.zeros_like(shadow)
    residual = shadow
    search = shadow
    rho_now = lax.psum(local_dot(shadow, shadow), ("wide", "narrow")) / total_cells
    for iteration in range(ITERS):
        search_image = operate(search, conductance, shift_col)
        denominator = lax.psum(local_dot(shadow, search_image), ("wide", "narrow")) / total_cells
        step_alpha = rho_now / denominator
        halfway = residual - spread(step_alpha) * search_image
        halfway_image = operate(halfway, conductance, shift_col)
        cross_sum, square_sum, shadow_half, shadow_image = lax.psum(
            (
                local_dot(halfway_image, halfway),
                local_dot(halfway_image, halfway_image),
                local_dot(shadow, halfway),
                local_dot(shadow, halfway_image),
            ),
            ("wide", "narrow"),
        )
        step_omega = cross_sum / total_cells / (square_sum / total_cells + 1e-06)
        solution = solution + spread(step_alpha) * search + spread(step_omega) * halfway
        residual = halfway - spread(step_omega) * halfway_image
        rho_next = shadow_half / total_cells - step_omega * (shadow_image / total_cells)
        if iteration + 1 < ITERS:
            step_beta = rho_next / rho_now * (step_alpha / step_omega)
            search = residual + spread(step_beta) * (search - spread(step_omega) * search_image)
            rho_now = rho_next
    vflat = old_basis.reshape(old_basis.shape[0], -1)
    wflat = solution.reshape(columns, -1)
    high = lax.Precision.HIGHEST
    first_coef = (
        lax.psum(jnp.einsum("bc,kc->bk", vflat, wflat, precision=high), ("wide", "narrow"))
        / total_cells
    )
    once = wflat - jnp.einsum("bk,bc->kc", first_coef, vflat, precision=high)
    second_coef = (
        lax.psum(jnp.einsum("bc,kc->bk", vflat, once, precision=high), ("wide", "narrow"))
        / total_cells
    )
    twice = once - jnp.einsum("bk,bc->kc", second_coef, vflat, precision=high)
    mean_square = lax.psum(jnp.sum(twice * twice, axis=1), ("wide", "narrow")) / total_cells
    col_scale = jnp.sqrt(mean_square + 1e-06)
    new_columns = (twice / col_scale[:, None]).reshape(solution.shape)
    return (new_columns, first_coef + second_coef, col_scale)


def solution(mesh):
    in_specs = (
        P(None, "wide", "narrow", None),
        P(None, "wide", "narrow", None),
        P("wide", "narrow", None),
        P(),
    )
    out_specs = (P(None, "wide", "narrow", None), P(), P())
    return jax.shard_map(shards, mesh=mesh, in_specs=in_specs, out_specs=out_specs, check_vma=False)
```

profile of v0, /device:TPU:0, one launch (start us, length us, event | category | flops | bytes accessed | tf_op | source)
XLA Modules:
  0.0 634.8 jit_solution(9891462262970364943)
XLA Ops:
  1.9 4.9 collective-permute-start.1
  8.1 2.8 collective-permute-done.1
  10.9 6.2 collective-permute-done
  17.1 1.3 collective-permute-start.3
  20.2 1.5 collective-permute-done.2
  23.1 40.2 %all-reduce.12 = (f32[48]{0:T(128)S(1)}, f32[48]{0:T(128)S(1)}) all-reduce(f32[48]{0:T(128)S(1)} %get-tuple-element.50, f32[48]{0:T(128)S(1)} %reduce_sum.183), channel_id=1, replica_groups=mesh['wide'=16,'narrow'=2] {'wide','narrow'}, use_global_device_ids=true, to_apply=%region_3.4 | all-reduce | flops 96 | bytes 768 | tf_op jit(solution)/shard_map/psum | solution.py:65
  63.5 4.2 collective-permute-start.5
  69.0 6.1 collective-permute-done.5
  75.1 1.9 collective-permute-done.4
  77.0 1.3 collective-permute-start.7
  79.6 2.0 collective-permute-done.6
  83.2 39.4 %all-reduce.11 = (f32[48]{0:T(128)S(1)}, f32[48]{0:T(128)S(1)}, f32[48]{0:T(128)S(1)}, f32[48]{0:T(128)S(1)}) all-reduce(f32[48]{0:T(128)S(1)} %get-tuple-element.4, f32[48]{0:T(128)S(1)} %get-tuple-element.6, f32[48]{0:T(128)S(1)} %get-tuple-element.5, ...), channel_id=1, replica_groups=mesh['wide'=16,'narrow'=2] {'wide','narrow'}, use_global_device_ids=true, to_apply=%region_5.6 | all-reduce | flops 192 | bytes 1536 | tf_op jit(solution)/shard_map/psum | solution.py:69
  122.9 4.2 collective-permute-start.9
  128.4 6.1 collective-permute-done.9
  134.5 1.9 collective-permute-done.8
  136.4 1.3 collective-permute-start.11
  139.0 2.0 collective-permute-done.10
  142.4 38.4 %psum.160 = f32[48]{0:T(128)S(1)} all-reduce(f32[48]{0:T(128)S(1)} %get-tuple-element.44), channel_id=1, replica_groups=mesh['wide'=16,'narrow'=2] {'wide','narrow'}, use_global_device_ids=true, to_apply=%region_13.14 | all-reduce | flops 48 | bytes 384 | tf_op jit(solution)/shard_map/psum | solution.py:65
  180.8 1.4 multiply_subtract_fusion.4
  182.2 4.2 collective-permute-start.13
  187.7 1.9 collective-permute-done.13
  189.5 5.9 collective-permute-done.12
  195.5 1.3 collective-permute-start.15
  198.1 2.0 collective-permute-done.14
  200.9 1.6 fusion.32
  202.5 39.3 %all-reduce.10 = (f32[48]{0:T(128)S(1)}, f32[48]{0:T(128)S(1)}, f32[48]{0:T(128)S(1)}, f32[48]{0:T(128)S(1)}) all-reduce(f32[48]{0:T(128)S(1)} %get-tuple-element.14, f32[48]{0:T(128)S(1)} %get-tuple-element.16, f32[48]{0:T(128)S(1)} %get-tuple-element.15, ...), channel_id=1, replica_groups=mesh['wide'=16,'narrow'=2] {'wide','narrow'}, use_global_device_ids=true, to_apply=%region_15.16 | all-reduce | flops 192 | bytes 1536 | tf_op jit(solution)/shard_map/psum | solution.py:69
  241.9 1.4 multiply_add_fusion.1
  243.3 4.2 collective-permute-start.17
  248.8 6.1 collective-permute-done.17
  254.9 1.9 collective-permute-done.16
  256.8 1.3 collective-permute-start.19
  258.1 1.5 collective-permute-start.18
  259.6 1.8 collective-permute-done.18
  262.2 1.4 fusion.34
  263.6 38.4 %psum.165 = f32[48]{0:T(128)S(1)} all-reduce(f32[48]{0:T(128)S(1)} %get-tuple-element.38), channel_id=1, replica_groups=mesh['wide'=16,'narrow'=2] {'wide','narrow'}, use_global_device_ids=true, to_apply=%region_23.24 | all-reduce | flops 48 | bytes 384 | tf_op jit(solution)/shard_map/psum | solution.py:65
  302.0 1.6 multiply_subtract_fusion.2
  303.6 4.2 collective-permute-start.21
  309.1 1.9 collective-permute-done.21
  310.9 5.9 collective-permute-done.20
  316.9 1.3 collective-permute-start.23
  319.5 2.0 collective-permute-done.22
  322.3 1.6 fusion.35
  323.9 39.3 %all-reduce.9 = (f32[48]{0:T(128)S(1)}, f32[48]{0:T(128)S(1)}, f32[48]{0:T(128)S(1)}, f32[48]{0:T(128)S(1)}) all-reduce(f32[48]{0:T(128)S(1)} %get-tuple-element.10, f32[48]{0:T(128)S(1)} %get-tuple-element.12, f32[48]{0:T(128)S(1)} %get-tuple-element.11, ...), channel_id=1, replica_groups=mesh['wide'=16,'narrow'=2] {'wide','narrow'}, use_global_device_ids=true, to_apply=%region_25.26 | all-reduce | flops 192 | bytes 1536 | tf_op jit(solution)/shard_map/psum | solution.py:69
  363.2 1.6 multiply_add_fusion
  364.9 4.2 collective-permute-start.25
  370.4 6.1 collective-permute-done.25
  376.5 1.9 collective-permute-done.24
  381.0 2.0 collective-permute-done.26
  383.8 1.4 fusion.37
  385.2 38.4 %psum.170 = f32[48]{0:T(128)S(1)} all-reduce(f32[48]{0:T(128)S(1)} %get-tuple-element.33), channel_id=1, replica_groups=mesh['wide'=16,'narrow'=2] {'wide','narrow'}, use_global_device_ids=true, to_apply=%region_33.34 | all-reduce | flops 48 | bytes 384 | tf_op jit(solution)/shard_map/psum | solution.py:65
  423.6 1.6 multiply_subtract_fusion
  425.2 4.2 collective-permute-start.29
  430.7 1.9 collective-permute-done.29
  432.6 5.9 collective-permute-done.28
  441.1 2.0 collective-permute-done.30
  444.5 39.3 %all-reduce.8 = (f32[48]{0:T(128)S(1)}, f32[48]{0:T(128)S(1)}) all-reduce(f32[48]{0:T(128)S(1)} %get-tuple-element.8, f32[48]{0:T(128)S(1)} %get-tuple-element.7), channel_id=1, replica_groups=mesh['wide'=16,'narrow'=2] {'wide','narrow'}, use_global_device_ids=true, to_apply=%region_37.38 | all-reduce | flops 96 | bytes 768 | tf_op jit(solution)/shard_map/psum | solution.py:69
  483.8 2.3 fusion.26
  486.7 5.3 fusion.10
  492.0 40.2 %psum.173 = f32[256,48]{0,1:T(8,128)S(1)} all-reduce(f32[256,48]{0,1:T(8,128)S(1)} %fusion.10), channel_id=1, replica_groups=mesh['wide'=16,'narrow'=2] {'wide','narrow'}, use_global_device_ids=true, to_apply=%region_38.39 | all-reduce | flops 12288 | bytes 98304 | tf_op jit(solution)/shard_map/psum | solution.py:90
  532.2 7.3 %convolution_subtract_fusion.1 = f32[48,4096]{1,0:T(8,128)S(1)} fusion(f32[32,8,32,128]{3,2,1,0:T(8,128)} %bitcast.104, f32[6,8,32,128]{3,2,1,0:T(8,128)S(1)} %bitcast.111, f32[256,48]{0,1:T(8,128)S(1)} %psum.173), kind=kOutput, calls=%fused_computation.16 | convolution fusion | flops 604188672 | bytes 5816320 | tf_op jit(solution)/shard_map/bk,bc->kc/dot_general | solution.py:93
  539.6 5.3 fusion.13
  544.9 41.0 %psum.174 = f32[256,48]{0,1:T(8,128)S(1)} all-reduce(f32[256,48]{0,1:T(8,128)S(1)} %fusion.13), channel_id=1, replica_groups=mesh['wide'=16,'narrow'=2] {'wide','narrow'}, use_global_device_ids=true, to_apply=%region_39.40 | all-reduce | flops 12288 | bytes 98304 | tf_op jit(solution)/shard_map/psum | solution.py:95
  586.6 7.0 %multiply_reduce_fusion = (f32[48]{0:T(128)S(1)}, f32[48,4096]{1,0:T(8,128)S(1)}) fusion(f32[48,4096]{1,0:T(8,128)S(1)} %convolution_subtract_fusion.1, f32[32,8,32,128]{3,2,1,0:T(8,128)} %bitcast.105, f32[256,48]{0,1:T(8,128)S(1)} %psum.174), kind=kOutput, calls=%fused_computation.211 | convolution fusion | flops 604581824 | bytes 5816512 | tf_op jit(solution)/shard_map/bk,bc->kc/dot_general | solution.py:98
  593.6 39.6 %psum.175 = f32[48]{0:T(128)S(1)} all-reduce(f32[48]{0:T(128)S(1)} %get-tuple-element.84), channel_id=1, replica_groups=mesh['wide'=16,'narrow'=2] {'wide','narrow'}, use_global_device_ids=true, to_apply=%region_41.42 | all-reduce | flops 48 | bytes 384 | tf_op jit(solution)/shard_map/psum | solution.py:99
  (95 shorter events, 36.0 us)
Async XLA Ops:
  0.6 19.1 %copy-start.6 = (f32[16,4,8,128]{3,2,1,0:T(8,128)S(1)}, f32[16,4,8,128]{3,2,1,0:T(8,128)}, u32[]{:S(2)}) copy-start(f32[16,4,8,128]{3,2,1,0:T(8,128)} %param.4) | copy-start | bytes 786436
  0.6 19.2 %copy-start.9 = (f32[3]{0:T(128)S(1)}, f32[3]{0:T(128)}, u32[]{:S(2)}) copy-start(f32[3]{0:T(128)} %param.7) | copy-start | bytes 40
  1.9 9.0 %collective-permute-start.1 = (f32[48,1,8,128]{3,0,2,1:T(8,128)S(1)}, f32[48,1,8,128]{3,0,2,1:T(8,128)S(1)}, u32[]{:S(2)}, u32[]{:S(2)}) collective-permute-start(f32[48,1,8,128]{3,0,2,1:T(8,128)S(1)} %get-tuple-element.82), channel_id=1, source_target_pairs={{0,2},{2,4},{4,6},{6,8},{8,10},{10,12},{12,14},{14,16},{16,18},{18... | collective-permute-start | bytes 589832 | tf_op jit(solution)/shard_map/ppermute | solution.py:17
  6.8 10.3 %collective-permute-start = (f32[48,1,8,128]{3,0,2,1:T(8,128)S(1)}, f32[48,1,8,128]{3,0,2,1:T(8,128)S(1)}, u32[]{:S(2)}, u32[]{:S(2)}) collective-permute-start(f32[48,1,8,128]{3,0,2,1:T(8,128)S(1)} %get-tuple-element.83), channel_id=1, source_target_pairs={{2,0},{4,2},{6,4},{8,6},{10,8},{12,10},{14,12},{16,14},{18,16},{20... | collective-permute-start | bytes 589832 | tf_op jit(solution)/shard_map/ppermute | solution.py:19
  17.1 5.4 copy-start.7
  17.1 3.1 collective-permute-start.3
  18.4 3.3 collective-permute-start.2
  23.1 157.7 %copy-start.2 = (f32[48,4,8,128]{3,0,2,1:T(8,128)}, f32[48,4,8,128]{3,0,2,1:T(8,128)S(1)}, u32[]{:S(2)}) copy-start(f32[48,4,8,128]{3,0,2,1:T(8,128)S(1)} %get-tuple-element.51) | copy-start | bytes 2359300
  63.5 11.6 %collective-permute-start.5 = (f32[48,1,8,128]{3,0,2,1:T(8,128)S(1)}, f32[48,1,8,128]{3,0,2,1:T(8,128)S(1)}, u32[]{:S(2)}, u32[]{:S(2)}) collective-permute-start(f32[48,1,8,128]{3,0,2,1:T(8,128)S(1)} %get-tuple-element.80), channel_id=1, source_target_pairs={{0,2},{2,4},{4,6},{6,8},{8,10},{10,12},{12,14},{14,16},{16,18},{18... | collective-permute-start | bytes 589832 | tf_op jit(solution)/shard_map/ppermute | solution.py:17
  67.7 9.3 %collective-permute-start.4 = (f32[48,1,8,128]{3,0,2,1:T(8,128)S(1)}, f32[48,1,8,128]{3,0,2,1:T(8,128)S(1)}, u32[]{:S(2)}, u32[]{:S(2)}) collective-permute-start(f32[48,1,8,128]{3,0,2,1:T(8,128)S(1)} %get-tuple-element.81), channel_id=1, source_target_pairs={{2,0},{4,2},{6,4},{8,6},{10,8},{12,10},{14,12},{16,14},{18,16},{20... | collective-permute-start | bytes 589832 | tf_op jit(solution)/shard_map/ppermute | solution.py:19
  77.0 2.6 collective-permute-start.7
  78.3 3.3 collective-permute-start.6
  83.2 58.6 %copy-start.5 = (f32[48,4,8,128]{3,0,2,1:T(8,128)}, f32[48,4,8,128]{3,0,2,1:T(8,128)S(1)}, u32[]{:S(2)}) copy-start(f32[48,4,8,128]{3,0,2,1:T(8,128)S(1)} %get-tuple-element.49) | copy-start | bytes 2359300
  122.9 11.6 %collective-permute-start.9 = (f32[48,1,8,128]{3,0,2,1:T(8,128)S(1)}, f32[48,1,8,128]{3,0,2,1:T(8,128)S(1)}, u32[]{:S(2)}, u32[]{:S(2)}) collective-permute-start(f32[48,1,8,128]{3,0,2,1:T(8,128)S(1)} %get-tuple-element.78), channel_id=1, source_target_pairs={{0,2},{2,4},{4,6},{6,8},{8,10},{10,12},{12,14},{14,16},{16,18},{18... | collective-permute-start | bytes 589832 | tf_op jit(solution)/shard_map/ppermute | solution.py:17
  127.1 9.3 %collective-permute-start.8 = (f32[48,1,8,128]{3,0,2,1:T(8,128)S(1)}, f32[48,1,8,128]{3,0,2,1:T(8,128)S(1)}, u32[]{:S(2)}, u32[]{:S(2)}) collective-permute-start(f32[48,1,8,128]{3,0,2,1:T(8,128)S(1)} %get-tuple-element.79), channel_id=1, source_target_pairs={{2,0},{4,2},{6,4},{8,6},{10,8},{12,10},{14,12},{16,14},{18,16},{20... | collective-permute-start | bytes 589832 | tf_op jit(solution)/shard_map/ppermute | solution.py:19
  136.4 2.6 collective-permute-start.11
  137.7 3.3 collective-permute-start.10
  182.2 7.4 %collective-permute-start.13 = (f32[48,1,8,128]{3,0,2,1:T(8,128)S(1)}, f32[48,1,8,128]{3,0,2,1:T(8,128)S(1)}, u32[]{:S(2)}, u32[]{:S(2)}) collective-permute-start(f32[48,1,8,128]{3,0,2,1:T(8,128)S(1)} %get-tuple-element.76), channel_id=1, source_target_pairs={{0,2},{2,4},{4,6},{6,8},{8,10},{10,12},{12,14},{14,16},{16,18},{18... | collective-permute-start | bytes 589832 | tf_op jit(solution)/shard_map/ppermute | solution.py:17
  186.4 9.1 %collective-permute-start.12 = (f32[48,1,8,128]{3,0,2,1:T(8,128)S(1)}, f32[48,1,8,128]{3,0,2,1:T(8,128)S(1)}, u32[]{:S(2)}, u32[]{:S(2)}) collective-permute-start(f32[48,1,8,128]{3,0,2,1:T(8,128)S(1)} %get-tuple-element.77), channel_id=1, source_target_pairs={{2,0},{4,2},{6,4},{8,6},{10,8},{12,10},{14,12},{16,14},{18,16},{20... | collective-permute-start | bytes 589832 | tf_op jit(solution)/shard_map/ppermute | solution.py:19
  195.5 2.6 collective-permute-start.15
  196.8 3.3 collective-permute-start.14
  243.3 11.6 %collective-permute-start.17 = (f32[48,1,8,128]{3,0,2,1:T(8,128)S(1)}, f32[48,1,8,128]{3,0,2,1:T(8,128)S(1)}, u32[]{:S(2)}, u32[]{:S(2)}) collective-permute-start(f32[48,1,8,128]{3,0,2,1:T(8,128)S(1)} %get-tuple-element.74), channel_id=1, source_target_pairs={{0,2},{2,4},{4,6},{6,8},{8,10},{10,12},{12,14},{14,16},{16,18},{18... | collective-permute-start | bytes 589832 | tf_op jit(solution)/shard_map/ppermute | solution.py:17
  247.5 9.3 %collective-permute-start.16 = (f32[48,1,8,128]{3,0,2,1:T(8,128)S(1)}, f32[48,1,8,128]{3,0,2,1:T(8,128)S(1)}, u32[]{:S(2)}, u32[]{:S(2)}) collective-permute-start(f32[48,1,8,128]{3,0,2,1:T(8,128)S(1)} %get-tuple-element.75), channel_id=1, source_target_pairs={{2,0},{4,2},{6,4},{8,6},{10,8},{12,10},{14,12},{16,14},{18,16},{20... | collective-permute-start | bytes 589832 | tf_op jit(solution)/shard_map/ppermute | solution.py:19
  256.8 2.8 collective-permute-start.19
  258.1 3.3 collective-permute-start.18
  303.6 7.4 %collective-permute-start.21 = (f32[48,1,8,128]{3,0,2,1:T(8,128)S(1)}, f32[48,1,8,128]{3,0,2,1:T(8,128)S(1)}, u32[]{:S(2)}, u32[]{:S(2)}) collective-permute-start(f32[48,1,8,128]{3,0,2,1:T(8,128)S(1)} %get-tuple-element.72), channel_id=1, source_target_pairs={{0,2},{2,4},{4,6},{6,8},{8,10},{10,12},{12,14},{14,16},{16,18},{18... | collective-permute-start | bytes 589832 | tf_op jit(solution)/shard_map/ppermute | solution.py:17
  307.8 9.1 %collective-permute-start.20 = (f32[48,1,8,128]{3,0,2,1:T(8,128)S(1)}, f32[48,1,8,128]{3,0,2,1:T(8,128)S(1)}, u32[]{:S(2)}, u32[]{:S(2)}) collective-permute-start(f32[48,1,8,128]{3,0,2,1:T(8,128)S(1)} %get-tuple-element.73), channel_id=1, source_target_pairs={{2,0},{4,2},{6,4},{8,6},{10,8},{12,10},{14,12},{16,14},{18,16},{20... | collective-permute-start | bytes 589832 | tf_op jit(solution)/shard_map/ppermute | solution.py:19
  316.9 2.6 collective-permute-start.23
  318.2 3.3 collective-permute-start.22
  364.9 19.0 %copy-start.3 = (f32[48,4,8,128]{3,0,2,1:T(8,128)}, f32[48,4,8,128]{3,0,2,1:T(8,128)S(1)}, u32[]{:S(2)}) copy-start(f32[48,4,8,128]{3,0,2,1:T(8,128)S(1)} %multiply_add_fusion) | copy-start | bytes 2359300
  364.9 11.6 %collective-permute-start.25 = (f32[48,1,8,128]{3,0,2,1:T(8,128)S(1)}, f32[48,1,8,128]{3,0,2,1:T(8,128)S(1)}, u32[]{:S(2)}, u32[]{:S(2)}) collective-permute-start(f32[48,1,8,128]{3,0,2,1:T(8,128)S(1)} %get-tuple-element.70), channel_id=1, source_target_pairs={{0,2},{2,4},{4,6},{6,8},{8,10},{10,12},{12,14},{14,16},{16,18},{18... | collective-permute-start | bytes 589832 | tf_op jit(solution)/shard_map/ppermute | solution.py:17
  369.1 9.3 %collective-permute-start.24 = (f32[48,1,8,128]{3,0,2,1:T(8,128)S(1)}, f32[48,1,8,128]{3,0,2,1:T(8,128)S(1)}, u32[]{:S(2)}, u32[]{:S(2)}) collective-permute-start(f32[48,1,8,128]{3,0,2,1:T(8,128)S(1)} %get-tuple-element.71), channel_id=1, source_target_pairs={{2,0},{4,2},{6,4},{8,6},{10,8},{12,10},{14,12},{16,14},{18,16},{20... | collective-permute-start | bytes 589832 | tf_op jit(solution)/shard_map/ppermute | solution.py:19
  378.4 2.6 collective-permute-start.27
  379.7 3.3 collective-permute-start.26
  425.2 18.8 %copy-start.4 = (f32[48,4,8,128]{3,0,2,1:T(8,128)}, f32[48,4,8,128]{3,0,2,1:T(8,128)S(1)}, u32[]{:S(2)}) copy-start(f32[48,4,8,128]{3,0,2,1:T(8,128)S(1)} %multiply_subtract_fusion) | copy-start | bytes 2359300
  425.2 7.4 %collective-permute-start.29 = (f32[48,1,8,128]{3,0,2,1:T(8,128)S(1)}, f32[48,1,8,128]{3,0,2,1:T(8,128)S(1)}, u32[]{:S(2)}, u32[]{:S(2)}) collective-permute-start(f32[48,1,8,128]{3,0,2,1:T(8,128)S(1)} %get-tuple-element.68), channel_id=1, source_target_pairs={{0,2},{2,4},{4,6},{6,8},{8,10},{10,12},{12,14},{14,16},{16,18},{18... | collective-permute-start | bytes 589832 | tf_op jit(solution)/shard_map/ppermute | solution.py:17
  429.4 9.1 %collective-permute-start.28 = (f32[48,1,8,128]{3,0,2,1:T(8,128)S(1)}, f32[48,1,8,128]{3,0,2,1:T(8,128)S(1)}, u32[]{:S(2)}, u32[]{:S(2)}) collective-permute-start(f32[48,1,8,128]{3,0,2,1:T(8,128)S(1)} %get-tuple-element.69), channel_id=1, source_target_pairs={{2,0},{4,2},{6,4},{8,6},{10,8},{12,10},{14,12},{16,14},{18,16},{20... | collective-permute-start | bytes 589832 | tf_op jit(solution)/shard_map/ppermute | solution.py:19
  438.5 2.6 collective-permute-start.31
  439.8 3.3 collective-permute-start.30
  483.8 2.9 copy-start
  532.2 7.3 %copy-start.1 = (f32[256,4,8,128]{3,2,1,0:T(8,128)S(1)}, f32[256,4,8,128]{3,2,1,0:T(8,128)}, u32[]{:S(2)}) copy-start(f32[256,4,8,128]{3,2,1,0:T(8,128)} %param.5) | copy-start | bytes 12582916
  633.2 1.2 copy-start.8
where the time goes:
time: 646 us; the launch traced here: 635 us
  blocking collectives  433 us (67%)
  waiting for transfers between devices  79.2 us (12%)
  starting transfers between devices  65.5 us (10%)
  other arithmetic  26.5 us (4%)
  matrix products  25 us (4%)
    psum x4, blocking collectives, shards(): lax.psum((local_dot(halfway_image, halfway), local_dot(halfway_image, hal...  157 us
    psum x4, blocking collectives, shards(): lax.psum(local_dot(shadow, search_image), ('wide', 'narrow')) / total_cells  155 us
    ppermute x16, waiting for transfers between devices, padded_2(): lax.ppermute(head, axis, [((i + 1) % count, i) for i in range(ends)])  46.5 us
    ppermute x16, starting transfers between devices, padded_2(): lax.ppermute(tail, axis, [(i, (i + 1) % count) for i in range(ends)])  44.6 us
    psum x1, blocking collectives, shards(): lax.psum(jnp.einsum('bc,kc->bk', vflat, once, precision=high), ('wide', '...  41 us
    psum x1, blocking collectives, shards(): lax.psum(jnp.einsum('bc,kc->bk', vflat, wflat, precision=high), ('wide',...  40.2 us
    psum x1, blocking collectives, shards(): lax.psum(jnp.sum(twice * twice, axis=1), ('wide', 'narrow')) / total_cells  39.6 us
    ppermute x16, waiting for transfers between devices, padded_2(): lax.ppermute(tail, axis, [(i, (i + 1) % count) for i in range(ends)])  32.8 us
  transfers between devices with their start and end apart: 32, of which 24 were waited for; matrix products, arithmetic and copies ran while one was open for 0% of the time, Pallas kernels for 0%

commit v1 on v0

--- a/solution.py
+++ b/solution.py
@@ -4,6 +4,12 @@
 from jax.sharding import PartitionSpec as P
 
 ITERS = 4
+
+
+def gather_and_add(x, axis):
+    parts = lax.all_gather(x, axis, axis=0, tiled=False)
+    acc = parts.sum(axis=0)
+    return acc
 
 
 def padded_2(cells, sides, width):
@@ -87,7 +93,7 @@
     wflat = solution.reshape(columns, -1)
     high = lax.Precision.HIGHEST
     first_coef = (
-        lax.psum(jnp.einsum("bc,kc->bk", vflat, wflat, precision=high), ("wide", "narrow"))
+        gather_and_add(jnp.einsum("bc,kc->bk", vflat, wflat, precision=high), ("wide", "narrow"))
         / total_cells
     )
     once = wflat - jnp.einsum("bk,bc->kc", first_coef, vflat, precision=high)

time: 646 us -> 673 us (1.042)
  waiting for transfers between devices: 79.2 us -> 131 us
  blocking collectives: 433 us -> 392 us
  between operations: 1.79 us -> 15 us
    all_gather x0 -> x1, waiting for transfers between devices: none -> 52.1 us  [gather_and_add(): parts = lax.all_gather(x, axis, axis=0, tiled=False)]
    psum x1 -> x0, blocking collectives: 40.2 us -> none  [shards(): lax.psum(jnp.einsum('bc,kc->bk', vflat, wflat, precision=high), ('wide',...]
  transfers between devices with their start and end apart: 32 -> 33, of which waited for: 24 -> 25; matrix products, arithmetic and copies ran while one was open for 0% -> 0% of each run, Pallas kernels for 0% -> 0%
where the time goes in v1:
time: 673 us; the launch traced here: 662 us
  blocking collectives  392 us (58%)
  waiting for transfers between devices  131 us (19%)
  starting transfers between devices  65.8 us (10%)
  other arithmetic  26.7 us (4%)
  matrix products  23.6 us (4%)
  between operations  15 us (2%)
  local copies, waits for them, and re-layouts  7.49 us (1%)
    psum x4, blocking collectives, shards(): lax.psum((local_dot(halfway_image, halfway), local_dot(halfway_image, hal...  157 us
    psum x4, blocking collectives, shards(): lax.psum(local_dot(shadow, search_image), ('wide', 'narrow')) / total_cells  155 us
    all_gather x1, waiting for transfers between devices, gather_and_add(): parts = lax.all_gather(x, axis, axis=0, tiled=False)  52.1 us
    ppermute x16, waiting for transfers between devices, padded_2(): lax.ppermute(head, axis, [((i + 1) % count, i) for i in range(ends)])  46.2 us
    ppermute x16, starting transfers between devices, padded_2(): lax.ppermute(tail, axis, [(i, (i + 1) % count) for i in range(ends)])  44.6 us
    psum x1, blocking collectives, shards(): lax.psum(jnp.einsum('bc,kc->bk', vflat, once, precision=high), ('wide', '...  40.2 us
    psum x1, blocking collectives, shards(): lax.psum(jnp.sum(twice * twice, axis=1), ('wide', 'narrow')) / total_cells  39.1 us
    ppermute x16, waiting for transfers between devices, padded_2(): lax.ppermute(tail, axis, [(i, (i + 1) % count) for i in range(ends)])  32.7 us
  transfers between devices with their start and end apart: 33, of which 25 were waited for; matrix products, arithmetic and copies ran while one was open for 0% of the time, Pallas kernels for 0%

profile of v1, /device:TPU:0, one launch (start us, length us, event | category | flops | bytes accessed | tf_op | source)
XLA Modules:
  0.0 661.8 jit_solution(8546289106400398968)
XLA Ops:
  8.5 4.9 collective-permute-start.1
  14.7 2.8 collective-permute-done.1
  17.5 6.2 collective-permute-done
  23.7 1.3 collective-permute-start.3
  26.8 1.5 collective-permute-done.2
  29.6 40.2 %all-reduce.12 = (f32[48]{0:T(128)S(1)}, f32[48]{0:T(128)S(1)}) all-reduce(f32[48]{0:T(128)S(1)} %get-tuple-element.50, f32[48]{0:T(128)S(1)} %reduce_sum.192), channel_id=1, replica_groups=mesh['wide'=16,'narrow'=2] {'wide','narrow'}, use_global_device_ids=true, to_apply=%region_3.4 | all-reduce | flops 96 | bytes 768 | tf_op jit(solution)/shard_map/psum | solution.py:71
  70.1 4.2 collective-permute-start.5
  75.6 6.1 collective-permute-done.5
  81.7 1.9 collective-permute-done.4
  83.6 1.3 collective-permute-start.7
  86.2 2.0 collective-permute-done.6
  89.8 39.4 %all-reduce.11 = (f32[48]{0:T(128)S(1)}, f32[48]{0:T(128)S(1)}, f32[48]{0:T(128)S(1)}, f32[48]{0:T(128)S(1)}) all-reduce(f32[48]{0:T(128)S(1)} %get-tuple-element.4, f32[48]{0:T(128)S(1)} %get-tuple-element.6, f32[48]{0:T(128)S(1)} %get-tuple-element.5, ...), channel_id=1, replica_groups=mesh['wide'=16,'narrow'=2] {'wide','narrow'}, use_global_device_ids=true, to_apply=%region_5.6 | all-reduce | flops 192 | bytes 1536 | tf_op jit(solution)/shard_map/psum | solution.py:75
  129.5 4.2 collective-permute-start.9
  135.0 6.1 collective-permute-done.9
  141.0 1.9 collective-permute-done.8
  143.0 1.3 collective-permute-start.11
  145.6 2.0 collective-permute-done.10
  148.9 38.4 %psum.153 = f32[48]{0:T(128)S(1)} all-reduce(f32[48]{0:T(128)S(1)} %get-tuple-element.44), channel_id=1, replica_groups=mesh['wide'=16,'narrow'=2] {'wide','narrow'}, use_global_device_ids=true, to_apply=%region_13.14 | all-reduce | flops 48 | bytes 384 | tf_op jit(solution)/shard_map/psum | solution.py:71
  187.3 1.4 multiply_subtract_fusion.4
  188.7 4.2 collective-permute-start.13
  194.2 1.9 collective-permute-done.13
  196.1 5.9 collective-permute-done.12
  202.0 1.3 collective-permute-start.15
  204.6 2.0 collective-permute-done.14
  207.4 1.6 fusion.32
  209.1 39.3 %all-reduce.10 = (f32[48]{0:T(128)S(1)}, f32[48]{0:T(128)S(1)}, f32[48]{0:T(128)S(1)}, f32[48]{0:T(128)S(1)}) all-reduce(f32[48]{0:T(128)S(1)} %get-tuple-element.14, f32[48]{0:T(128)S(1)} %get-tuple-element.16, f32[48]{0:T(128)S(1)} %get-tuple-element.15, ...), channel_id=1, replica_groups=mesh['wide'=16,'narrow'=2] {'wide','narrow'}, use_global_device_ids=true, to_apply=%region_15.16 | all-reduce | flops 192 | bytes 1536 | tf_op jit(solution)/shard_map/psum | solution.py:75
  248.4 1.4 multiply_add_fusion.1
  249.8 4.2 collective-permute-start.17
  255.3 6.1 collective-permute-done.17
  261.4 1.9 collective-permute-done.16
  264.6 1.8 collective-permute-start.18
  266.4 1.5 collective-permute-done.18
  268.7 1.4 fusion.34
  270.1 38.4 %psum.158 = f32[48]{0:T(128)S(1)} all-reduce(f32[48]{0:T(128)S(1)} %get-tuple-element.38), channel_id=1, replica_groups=mesh['wide'=16,'narrow'=2] {'wide','narrow'}, use_global_device_ids=true, to_apply=%region_23.24 | all-reduce | flops 48 | bytes 384 | tf_op jit(solution)/shard_map/psum | solution.py:71
  308.5 1.6 multiply_subtract_fusion.2
  310.1 4.2 collective-permute-start.21
  315.6 1.9 collective-permute-done.21
  317.5 5.9 collective-permute-done.20
  326.0 2.0 collective-permute-done.22
  328.8 1.6 fusion.35
  330.5 39.3 %all-reduce.9 = (f32[48]{0:T(128)S(1)}, f32[48]{0:T(128)S(1)}, f32[48]{0:T(128)S(1)}, f32[48]{0:T(128)S(1)}) all-reduce(f32[48]{0:T(128)S(1)} %get-tuple-element.10, f32[48]{0:T(128)S(1)} %get-tuple-element.12, f32[48]{0:T(128)S(1)} %get-tuple-element.11, ...), channel_id=1, replica_groups=mesh['wide'=16,'narrow'=2] {'wide','narrow'}, use_global_device_ids=true, to_apply=%region_25.26 | all-reduce | flops 192 | bytes 1536 | tf_op jit(solution)/shard_map/psum | solution.py:75
  369.8 1.6 multiply_add_fusion
  371.4 4.2 collective-permute-start.25
  376.9 6.1 collective-permute-done.25
  383.0 1.9 collective-permute-done.24
  387.6 2.0 collective-permute-done.26
  390.4 1.4 fusion.37
  391.8 38.4 %psum.163 = f32[48]{0:T(128)S(1)} all-reduce(f32[48]{0:T(128)S(1)} %get-tuple-element.33), channel_id=1, replica_groups=mesh['wide'=16,'narrow'=2] {'wide','narrow'}, use_global_device_ids=true, to_apply=%region_33.34 | all-reduce | flops 48 | bytes 384 | tf_op jit(solution)/shard_map/psum | solution.py:71
  430.1 1.6 multiply_subtract_fusion
  431.7 4.2 collective-permute-start.29
  437.2 1.9 collective-permute-done.29
  439.1 5.9 collective-permute-done.28
  447.7 2.0 collective-permute-done.30
  451.0 39.4 %all-reduce.8 = (f32[48]{0:T(128)S(1)}, f32[48]{0:T(128)S(1)}) all-reduce(f32[48]{0:T(128)S(1)} %get-tuple-element.8, f32[48]{0:T(128)S(1)} %get-tuple-element.7), channel_id=1, replica_groups=mesh['wide'=16,'narrow'=2] {'wide','narrow'}, use_global_device_ids=true, to_apply=%region_37.38 | all-reduce | flops 96 | bytes 768 | tf_op jit(solution)/shard_map/psum | solution.py:75
  490.5 2.3 fusion.26
  493.7 6.0 fusion.10
  499.6 1.4 copy.11
  501.0 52.1 %all-gather.3.cloned.1.call-done = f32[8192,48]{0,1:T(8,128)} async-done(((f32[256,48]{0,1:T(8,128)}), f32[8192,48]{0,1:T(8,128)}) %all-gather.3.cloned.1.call-update) | async-done | bytes 1572880 | tf_op jit(solution)/shard_map/all_gather | solution.py:10
  553.2 2.0 copy.15
  555.8 5.1 convolution_subtract_fusion.1
  561.0 5.6 fusion.13
  566.5 40.2 %psum.166 = f32[256,48]{0,1:T(8,128)S(1)} all-reduce(f32[256,48]{0,1:T(8,128)S(1)} %fusion.13), channel_id=1, replica_groups=mesh['wide'=16,'narrow'=2] {'wide','narrow'}, use_global_device_ids=true, to_apply=%region_39.40 | all-reduce | flops 12288 | bytes 98304 | tf_op jit(solution)/shard_map/psum | solution.py:101
  607.4 7.0 %multiply_reduce_fusion = (f32[48]{0:T(128)S(1)}, f32[48,4096]{1,0:T(8,128)S(1)}) fusion(f32[48,4096]{1,0:T(8,128)S(1)} %convolution_subtract_fusion.1, f32[32,8,32,128]{3,2,1,0:T(8,128)} %bitcast.109, f32[256,48]{0,1:T(8,128)S(1)} %psum.166), kind=kOutput, calls=%fused_computation.212 | convolution fusion | flops 604581824 | bytes 5816512 | tf_op jit(solution)/shard_map/bk,bc->kc/dot_general | solution.py:104
  614.4 39.1 %psum.167 = f32[48]{0:T(128)S(1)} all-reduce(f32[48]{0:T(128)S(1)} %get-tuple-element.84), channel_id=1, replica_groups=mesh['wide'=16,'narrow'=2] {'wide','narrow'}, use_global_device_ids=true, to_apply=%region_41.42 | all-reduce | flops 48 | bytes 384 | tf_op jit(solution)/shard_map/psum | solution.py:105
  (101 shorter events, 39.5 us)
Async XLA Ops:
  7.2 19.1 %copy-start.7 = (f32[16,4,8,128]{3,2,1,0:T(8,128)S(1)}, f32[16,4,8,128]{3,2,1,0:T(8,128)}, u32[]{:S(2)}) copy-start(f32[16,4,8,128]{3,2,1,0:T(8,128)} %param.4) | copy-start | bytes 786436
  7.2 19.2 %copy-start.10 = (f32[3]{0:T(128)S(1)}, f32[3]{0:T(128)}, u32[]{:S(2)}) copy-start(f32[3]{0:T(128)} %param.7) | copy-start | bytes 40
  7.2 546.0 %all-gather.3.cloned.1.call-start = ((), (), s32[]{:S(2)}) async-start(), calls=%async_computation | async-start | bytes 1622016 | tf_op jit(solution)/shard_map/all_gather | solution.py:10
  8.5 9.0 %collective-permute-start.1 = (f32[48,1,8,128]{3,0,2,1:T(8,128)S(1)}, f32[48,1,8,128]{3,0,2,1:T(8,128)S(1)}, u32[]{:S(2)}, u32[]{:S(2)}) collective-permute-start(f32[48,1,8,128]{3,0,2,1:T(8,128)S(1)} %get-tuple-element.82), channel_id=1, source_target_pairs={{0,2},{2,4},{4,6},{6,8},{8,10},{10,12},{12,14},{14,16},{16,18},{18... | collective-permute-start | bytes 589832 | tf_op jit(solution)/shard_map/ppermute | solution.py:23
  13.4 10.3 %collective-permute-start = (f32[48,1,8,128]{3,0,2,1:T(8,128)S(1)}, f32[48,1,8,128]{3,0,2,1:T(8,128)S(1)}, u32[]{:S(2)}, u32[]{:S(2)}) collective-permute-start(f32[48,1,8,128]{3,0,2,1:T(8,128)S(1)} %get-tuple-element.83), channel_id=1, source_target_pairs={{2,0},{4,2},{6,4},{8,6},{10,8},{12,10},{14,12},{16,14},{18,16},{20... | collective-permute-start | bytes 589832 | tf_op jit(solution)/shard_map/ppermute | solution.py:25
  23.7 5.4 copy-start.8
  23.7 3.1 collective-permute-start.3
  25.0 3.3 collective-permute-start.2
  29.6 157.7 %copy-start.2 = (f32[48,4,8,128]{3,0,2,1:T(8,128)}, f32[48,4,8,128]{3,0,2,1:T(8,128)S(1)}, u32[]{:S(2)}) copy-start(f32[48,4,8,128]{3,0,2,1:T(8,128)S(1)} %get-tuple-element.51) | copy-start | bytes 2359300
  70.1 11.6 %collective-permute-start.5 = (f32[48,1,8,128]{3,0,2,1:T(8,128)S(1)}, f32[48,1,8,128]{3,0,2,1:T(8,128)S(1)}, u32[]{:S(2)}, u32[]{:S(2)}) collective-permute-start(f32[48,1,8,128]{3,0,2,1:T(8,128)S(1)} %get-tuple-element.80), channel_id=1, source_target_pairs={{0,2},{2,4},{4,6},{6,8},{8,10},{10,12},{12,14},{14,16},{16,18},{18... | collective-permute-start | bytes 589832 | tf_op jit(solution)/shard_map/ppermute | solution.py:23
  74.3 9.3 %collective-permute-start.4 = (f32[48,1,8,128]{3,0,2,1:T(8,128)S(1)}, f32[48,1,8,128]{3,0,2,1:T(8,128)S(1)}, u32[]{:S(2)}, u32[]{:S(2)}) collective-permute-start(f32[48,1,8,128]{3,0,2,1:T(8,128)S(1)} %get-tuple-element.81), channel_id=1, source_target_pairs={{2,0},{4,2},{6,4},{8,6},{10,8},{12,10},{14,12},{16,14},{18,16},{20... | collective-permute-start | bytes 589832 | tf_op jit(solution)/shard_map/ppermute | solution.py:25
  83.6 2.6 collective-permute-start.7
  84.9 3.3 collective-permute-start.6
  89.8 58.6 %copy-start.5 = (f32[48,4,8,128]{3,0,2,1:T(8,128)}, f32[48,4,8,128]{3,0,2,1:T(8,128)S(1)}, u32[]{:S(2)}) copy-start(f32[48,4,8,128]{3,0,2,1:T(8,128)S(1)} %get-tuple-element.49) | copy-start | bytes 2359300
  129.5 11.6 %collective-permute-start.9 = (f32[48,1,8,128]{3,0,2,1:T(8,128)S(1)}, f32[48,1,8,128]{3,0,2,1:T(8,128)S(1)}, u32[]{:S(2)}, u32[]{:S(2)}) collective-permute-start(f32[48,1,8,128]{3,0,2,1:T(8,128)S(1)} %get-tuple-element.78), channel_id=1, source_target_pairs={{0,2},{2,4},{4,6},{6,8},{8,10},{10,12},{12,14},{14,16},{16,18},{18... | collective-permute-start | bytes 589832 | tf_op jit(solution)/shard_map/ppermute | solution.py:23
  133.7 9.3 %collective-permute-start.8 = (f32[48,1,8,128]{3,0,2,1:T(8,128)S(1)}, f32[48,1,8,128]{3,0,2,1:T(8,128)S(1)}, u32[]{:S(2)}, u32[]{:S(2)}) collective-permute-start(f32[48,1,8,128]{3,0,2,1:T(8,128)S(1)} %get-tuple-element.79), channel_id=1, source_target_pairs={{2,0},{4,2},{6,4},{8,6},{10,8},{12,10},{14,12},{16,14},{18,16},{20... | collective-permute-start | bytes 589832 | tf_op jit(solution)/shard_map/ppermute | solution.py:25
  143.0 2.6 collective-permute-start.11
  144.3 3.3 collective-permute-start.10
  188.7 7.4 %collective-permute-start.13 = (f32[48,1,8,128]{3,0,2,1:T(8,128)S(1)}, f32[48,1,8,128]{3,0,2,1:T(8,128)S(1)}, u32[]{:S(2)}, u32[]{:S(2)}) collective-permute-start(f32[48,1,8,128]{3,0,2,1:T(8,128)S(1)} %get-tuple-element.76), channel_id=1, source_target_pairs={{0,2},{2,4},{4,6},{6,8},{8,10},{10,12},{12,14},{14,16},{16,18},{18... | collective-permute-start | bytes 589832 | tf_op jit(solution)/shard_map/ppermute | solution.py:23
  192.9 9.1 %collective-permute-start.12 = (f32[48,1,8,128]{3,0,2,1:T(8,128)S(1)}, f32[48,1,8,128]{3,0,2,1:T(8,128)S(1)}, u32[]{:S(2)}, u32[]{:S(2)}) collective-permute-start(f32[48,1,8,128]{3,0,2,1:T(8,128)S(1)} %get-tuple-element.77), channel_id=1, source_target_pairs={{2,0},{4,2},{6,4},{8,6},{10,8},{12,10},{14,12},{16,14},{18,16},{20... | collective-permute-start | bytes 589832 | tf_op jit(solution)/shard_map/ppermute | solution.py:25
  202.0 2.6 collective-permute-start.15
  203.3 3.3 collective-permute-start.14
  249.8 11.6 %collective-permute-start.17 = (f32[48,1,8,128]{3,0,2,1:T(8,128)S(1)}, f32[48,1,8,128]{3,0,2,1:T(8,128)S(1)}, u32[]{:S(2)}, u32[]{:S(2)}) collective-permute-start(f32[48,1,8,128]{3,0,2,1:T(8,128)S(1)} %get-tuple-element.74), channel_id=1, source_target_pairs={{0,2},{2,4},{4,6},{6,8},{8,10},{10,12},{12,14},{14,16},{16,18},{18... | collective-permute-start | bytes 589832 | tf_op jit(solution)/shard_map/ppermute | solution.py:23
  254.0 9.3 %collective-permute-start.16 = (f32[48,1,8,128]{3,0,2,1:T(8,128)S(1)}, f32[48,1,8,128]{3,0,2,1:T(8,128)S(1)}, u32[]{:S(2)}, u32[]{:S(2)}) collective-permute-start(f32[48,1,8,128]{3,0,2,1:T(8,128)S(1)} %get-tuple-element.75), channel_id=1, source_target_pairs={{2,0},{4,2},{6,4},{8,6},{10,8},{12,10},{14,12},{16,14},{18,16},{20... | collective-permute-start | bytes 589832 | tf_op jit(solution)/shard_map/ppermute | solution.py:25
  263.3 3.1 collective-permute-start.19
  264.6 3.3 collective-permute-start.18
  310.1 7.4 %collective-permute-start.21 = (f32[48,1,8,128]{3,0,2,1:T(8,128)S(1)}, f32[48,1,8,128]{3,0,2,1:T(8,128)S(1)}, u32[]{:S(2)}, u32[]{:S(2)}) collective-permute-start(f32[48,1,8,128]{3,0,2,1:T(8,128)S(1)} %get-tuple-element.72), channel_id=1, source_target_pairs={{0,2},{2,4},{4,6},{6,8},{8,10},{10,12},{12,14},{14,16},{16,18},{18... | collective-permute-start | bytes 589832 | tf_op jit(solution)/shard_map/ppermute | solution.py:23
  314.3 9.1 %collective-permute-start.20 = (f32[48,1,8,128]{3,0,2,1:T(8,128)S(1)}, f32[48,1,8,128]{3,0,2,1:T(8,128)S(1)}, u32[]{:S(2)}, u32[]{:S(2)}) collective-permute-start(f32[48,1,8,128]{3,0,2,1:T(8,128)S(1)} %get-tuple-element.73), channel_id=1, source_target_pairs={{2,0},{4,2},{6,4},{8,6},{10,8},{12,10},{14,12},{16,14},{18,16},{20... | collective-permute-start | bytes 589832 | tf_op jit(solution)/shard_map/ppermute | solution.py:25
  323.4 2.6 collective-permute-start.23
  324.7 3.3 collective-permute-start.22
  371.4 19.0 %copy-start.3 = (f32[48,4,8,128]{3,0,2,1:T(8,128)}, f32[48,4,8,128]{3,0,2,1:T(8,128)S(1)}, u32[]{:S(2)}) copy-start(f32[48,4,8,128]{3,0,2,1:T(8,128)S(1)} %multiply_add_fusion) | copy-start | bytes 2359300
  371.4 11.6 %collective-permute-start.25 = (f32[48,1,8,128]{3,0,2,1:T(8,128)S(1)}, f32[48,1,8,128]{3,0,2,1:T(8,128)S(1)}, u32[]{:S(2)}, u32[]{:S(2)}) collective-permute-start(f32[48,1,8,128]{3,0,2,1:T(8,128)S(1)} %get-tuple-element.70), channel_id=1, source_target_pairs={{0,2},{2,4},{4,6},{6,8},{8,10},{10,12},{12,14},{14,16},{16,18},{18... | collective-permute-start | bytes 589832 | tf_op jit(solution)/shard_map/ppermute | solution.py:23
  375.6 9.3 %collective-permute-start.24 = (f32[48,1,8,128]{3,0,2,1:T(8,128)S(1)}, f32[48,1,8,128]{3,0,2,1:T(8,128)S(1)}, u32[]{:S(2)}, u32[]{:S(2)}) collective-permute-start(f32[48,1,8,128]{3,0,2,1:T(8,128)S(1)} %get-tuple-element.71), channel_id=1, source_target_pairs={{2,0},{4,2},{6,4},{8,6},{10,8},{12,10},{14,12},{16,14},{18,16},{20... | collective-permute-start | bytes 589832 | tf_op jit(solution)/shard_map/ppermute | solution.py:25
  385.0 2.6 collective-permute-start.27
  386.3 3.3 collective-permute-start.26
  431.7 18.8 %copy-start.4 = (f32[48,4,8,128]{3,0,2,1:T(8,128)}, f32[48,4,8,128]{3,0,2,1:T(8,128)S(1)}, u32[]{:S(2)}) copy-start(f32[48,4,8,128]{3,0,2,1:T(8,128)S(1)} %multiply_subtract_fusion) | copy-start | bytes 2359300
  431.7 7.4 %collective-permute-start.29 = (f32[48,1,8,128]{3,0,2,1:T(8,128)S(1)}, f32[48,1,8,128]{3,0,2,1:T(8,128)S(1)}, u32[]{:S(2)}, u32[]{:S(2)}) collective-permute-start(f32[48,1,8,128]{3,0,2,1:T(8,128)S(1)} %get-tuple-element.68), channel_id=1, source_target_pairs={{0,2},{2,4},{4,6},{6,8},{8,10},{10,12},{12,14},{14,16},{16,18},{18... | collective-permute-start | bytes 589832 | tf_op jit(solution)/shard_map/ppermute | solution.py:23
  435.9 9.1 %collective-permute-start.28 = (f32[48,1,8,128]{3,0,2,1:T(8,128)S(1)}, f32[48,1,8,128]{3,0,2,1:T(8,128)S(1)}, u32[]{:S(2)}, u32[]{:S(2)}) collective-permute-start(f32[48,1,8,128]{3,0,2,1:T(8,128)S(1)} %get-tuple-element.69), channel_id=1, source_target_pairs={{2,0},{4,2},{6,4},{8,6},{10,8},{12,10},{14,12},{16,14},{18,16},{20... | collective-permute-start | bytes 589832 | tf_op jit(solution)/shard_map/ppermute | solution.py:25
  445.0 2.6 collective-permute-start.31
  446.4 3.3 collective-permute-start.30
  490.5 3.2 copy-start
  492.8 0.9 copy-start.6
  553.2 2.7 copy-start.1
  653.6 1.2 copy-start.9
Sparse Core Ops, SparseCore 0:
  499.8 53.3 all-gather.2
